TPU v7x, 32 devices: a whole 2x2x4 slice. The times are simulated.
32 devices in a mesh: ya: 8 (over z, y), zb: 4 (over x, core).
Axes of the slice: x: 2, y: 2, z: 4, core: 2. Of those that a mesh axis runs over, the one named last changes fastest.
Arguments:
- source: float32 [128, 128, 512], P(None, 'ya', 'zb'), may hold values from -6 to 6
- symbol_x: float32 [128], replicated, may hold values from 0.3 to 3
- symbol_y: float32 [128], replicated, may hold values from 0.3 to 3
- symbol_z: float32 [512], replicated, may hold values from 0.3 to 3
Outputs:
- modes: float32 [128, 128, 512], P('ya', 'zb')
All inputs are finite; a program needn't handle non-finite values.
Results may differ from a plain program's by a relative error of at most 0.000071.
Values sent between devices are 32-bit elements; how exact they have to be, the bound alone decides.
A program may use at most 64 MiB of HBM per device.

v0:
```python
import jax
import jax.numpy as jnp
from jax import lax
from jax.sharding import PartitionSpec as P


def transform_table(count):
    rank = jnp.arange(count)
    angle = (
        jnp.pi
        / (count + 1)
        * ((rank[:, None] + 1) * (rank[None, :] + 1) % (2 * count + 2)).astype(jnp.float32)
    )
    return jnp.sin(angle) * (2.0 / (count + 1)) ** 0.5


def transform_dim(values, dim):
    moved = jnp.tensordot(
        values,
        transform_table(values.shape[dim]),
        axes=([dim], [0]),
        precision=lax.Precision.HIGHEST,
    )
    return jnp.moveaxis(moved, -1, dim)


def body(source, symbol_x, symbol_y, symbol_z):
    part_values = source
    part_values = transform_dim(part_values, 0)
    part_values = lax.all_to_all(part_values, "ya", split_axis=0, concat_axis=1, tiled=True)
    part_values = transform_dim(part_values, 1)
    pencil_values = part_values
    pencil_values = lax.all_to_all(pencil_values, "zb", split_axis=1, concat_axis=2, tiled=True)
    pencil_values = transform_dim(pencil_values, 2)
    share_x = pencil_values.shape[0]
    part_x = lax.dynamic_slice_in_dim(symbol_x, lax.axis_index("ya") * share_x, share_x)
    share_y = pencil_values.shape[1]
    part_y = lax.dynamic_slice_in_dim(symbol_y, lax.axis_index("zb") * share_y, share_y)
    symbol = part_x[:, None, None] + part_y[None, :, None] + symbol_z[None, None, :]
    pencil_values = pencil_values * lax.rsqrt(symbol)
    return pencil_values


def solution(mesh):
    placed = (P(None, "ya", "zb"), P(), P(), P())
    return jax.shard_map(
        body, mesh=mesh, in_specs=placed, out_specs=P("ya", "zb", None), check_vma=False
    )
```

profile of v0, /device:TPU:0, one launch (start us, length us, event | category | flops | bytes accessed | tf_op | source)
XLA Modules:
  0.0 66.0 jit_solution(8343601692508259223)
XLA Ops:
  0.0 0.0 copy-start
  0.0 1.2 %copy-done = f32[128,16,128]{2,1,0:T(8,128)S(1)} copy-done((f32[128,16,128]{2,1,0:T(8,128)S(1)}, f32[128,16,128]{2,1,0:T(8,128)}, u32[]{:S(2)}) %copy-start) | copy-done | bytes 1048600
  1.2 1.6 %fusion.6 = f32[128,16,128]{2,0,1:T(8,128)S(1)} fusion(f32[128,16,128]{2,1,0:T(8,128)S(1)} %copy-done, s32[128]{0:T(128)S(1)} %iota_add_fusion.1), kind=kOutput, calls=%fused_computation.8 | convolution fusion | flops 402817024 | bytes 2097664 | tf_op jit(solution)/shard_map/dot_general | solution.py:18
  2.8 0.6 copy.24
  3.5 32.9 %all_to_all.36 = f32[128,16,128]{2,1,0:T(8,128)S(1)} all-to-all(f32[128,16,128]{2,1,0:T(8,128)S(1)} %copy.24), channel_id=1, replica_groups=mesh['ya'=8,'zb'=4] {'ya'}, dimensions={0} | all-to-all | bytes 2097152 | tf_op jit(solution)/shard_map/all_to_all | solution.py:30
  36.3 0.1 copy.25
  36.4 2.0 %convolution_bitcast_fusion = f32[16,128,128]{1,2,0:T(8,128)S(1)} fusion(f32[16,128,128]{2,1,0:T(8,128)S(1)} %bitcast.21, s32[128]{0:T(128)S(1)} %iota_add_fusion.1), kind=kOutput, calls=%fused_computation.2 | convolution fusion | flops 402817024 | bytes 2097664 | tf_op jit(solution)/shard_map/dot_general | solution.py:18
  38.4 1.4 %copy.27 = f32[16,128,128]{2,0,1:T(8,128)} copy(f32[16,128,128]{1,2,0:T(8,128)S(1)} %convolution_bitcast_fusion) | data formatting | bytes 2097152 | tf_op jit(solution)/shard_map/transpose | solution.py:24
  39.8 3.7 %all-to-all-start.1 = ((f32[16,128,128]{2,0,1:T(8,128)}), f32[16,128,128]{2,0,1:T(8,128)S(1)}, u32[]{:S(2)}, u32[]{:S(2)}) async-start(f32[16,128,128]{2,0,1:T(8,128)} %copy.27), calls=%async_computation.1 | async-start | bytes 2097152 | tf_op jit(solution)/shard_map/all_to_all | solution.py:33
  43.5 0.0 copy-start.2
  43.5 0.6 copy-done.2
  44.2 0.1 dynamic_slice.7
  44.2 0.0 copy-start.3
  44.2 0.7 copy-done.3
  44.9 0.1 dynamic_slice.6
  45.0 0.1 broadcast_add_fusion
  45.0 12.7 %all-to-all-done.1 = f32[16,128,128]{2,0,1:T(8,128)S(1)} async-done(((f32[16,128,128]{2,0,1:T(8,128)}), f32[16,128,128]{2,0,1:T(8,128)S(1)}, u32[]{:S(2)}, u32[]{:S(2)}) %all-to-all-start.1) | async-done | bytes 1048608 | tf_op jit(solution)/shard_map/all_to_all | solution.py:33
  57.7 0.7 %copy.29 = f32[16,32,4,128]{3,2,1,0:T(4,128)S(1)} copy(f32[16,32,4,128]{3,0,1,2:T(8,128)S(1)} %bitcast.19) | data formatting | bytes 2097152 | tf_op jit(solution)/shard_map/all_to_all | solution.py:33
  58.4 0.0 copy-start.1
  58.4 0.4 all_to_all.33
  58.8 0.2 copy-done.1
  59.1 6.9 %convolution_multiply_fusion = f32[16,32,512]{2,1,0:T(8,128)} fusion(f32[16,32,512]{2,1,0:T(8,128)S(1)} %all_to_all.33, f32[512]{0:T(512)S(1)} %copy-done.1, f32[16,32]{1,0:T(8,128)S(1)} %broadcast_add_fusion, s32[512]{0:T(512)S(1)} %iota_add_fusion), kind=kOutput, calls=%fused_computation.1 | convolution fusion | flops 1613758464 | bytes 2103296 | tf_op jit(solution)/shard_map/dot_general | solution.py:18
  (2 shorter events, 0.0 us)
Async XLA Ops:
  0.0 1.2 %copy-start = (f32[128,16,128]{2,1,0:T(8,128)S(1)}, f32[128,16,128]{2,1,0:T(8,128)}, u32[]{:S(2)}) copy-start(f32[128,16,128]{2,1,0:T(8,128)} %param.4) | copy-start | bytes 3145732
  39.8 17.9 %all-to-all-start.1 = ((f32[16,128,128]{2,0,1:T(8,128)}), f32[16,128,128]{2,0,1:T(8,128)S(1)}, u32[]{:S(2)}, u32[]{:S(2)}) async-start(f32[16,128,128]{2,0,1:T(8,128)} %copy.27), calls=%async_computation.1 | async-start | bytes 2097152 | tf_op jit(solution)/shard_map/all_to_all | solution.py:33
  43.5 0.7 copy-start.2
  44.2 0.7 copy-start.3
  58.4 0.7 %copy-start.1 = (f32[512]{0:T(512)S(1)}, f32[512]{0:T(512)}, u32[]{:S(2)}) copy-start(f32[512]{0:T(512)} %param.7) | copy-start | bytes 6148
where the time goes:
time: 66.3 us; the launch traced here: 66 us
  blocking collectives  32.9 us (50%)
  waiting for transfers between devices  12.7 us (19%)
  matrix products  10.5 us (16%)
  local copies, waits for them, and re-layouts  6.11 us (9%)
  starting transfers between devices  3.7 us (6%)
    all_to_all x1, blocking collectives, body(): lax.all_to_all(part_values, 'ya', split_axis=0, concat_axis=1, tiled=True)  32.9 us
    all_to_all x1, waiting for transfers between devices, body(): lax.all_to_all(pencil_values, 'zb', split_axis=1, concat_axis=2, tiled=True)  12.7 us
    dot_general x3, matrix products, transform_dim(): jnp.tensordot(values, transform_table(values.shape[dim]), axes=([dim], [0...  10.5 us
    all_to_all x1, starting transfers between devices, body(): lax.all_to_all(pencil_values, 'zb', split_axis=1, concat_axis=2, tiled=True)  3.7 us
    unnamed x8, local copies, waits for them, and re-layouts  2.77 us
    transpose x1, local copies, waits for them, and re-layouts, transform_dim(): return jnp.moveaxis(moved, -1, dim)  1.38 us
  transfers between devices with their start and end apart: 1, of which 1 were waited for; matrix products, arithmetic and copies ran while one was open for 0% of the time, Pallas kernels for 0%

commit v1 on v0

v1 whole, which is shorter than its diff:
```python
import functools

import jax
import jax.numpy as jnp
import numpy as np
from jax import lax
from jax.experimental import pallas as pl
from jax.experimental.pallas import tpu as pltpu
from jax.sharding import PartitionSpec as P

MESH = pl.DeviceIdType.MESH
CHUNKS = 4


def transform_table(count):
    rank = np.arange(1, count + 1)
    angle = np.pi / (count + 1) * (rank[:, None] * rank[None, :] % (2 * count + 2))
    table = np.sqrt(2.0 / (count + 1)) * np.sin(angle)
    high = table.astype(jnp.bfloat16)
    low = (table - high.astype(np.float64)).astype(jnp.bfloat16)
    return high, low


def halves(values):
    high = values.astype(jnp.bfloat16)
    return high, (values - high.astype(jnp.float32)).astype(jnp.bfloat16)


def left_product(table3, values):
    high, low = halves(values)
    stacked = jnp.concatenate([high, low, high], axis=0)
    return jnp.dot(table3, stacked, preferred_element_type=jnp.float32)


def partner(me, step, count):
    if count & (count - 1):
        return lax.rem(me + step, count)
    flipped, bit = 0, 1
    while bit < count:
        flipped = flipped + lax.rem(me // bit + step // bit, 2) * bit
        bit *= 2
    return flipped


def back(me, step, count):
    if count & (count - 1):
        return lax.rem(me + count - step, count)
    return partner(me, step, count)


def kernel(
    n_ya, n_zb, chunks,
    source, table_x, table_y, high_z, low_z,
    out,
    src, tx, ty, hz, lz, first, second, third, lines,
    load_sem, send_a, recv_a, send_b, recv_b,
):
    ya, zb = lax.axis_index("ya"), lax.axis_index("zb")
    nx, yl, zl = source.shape
    ny = yl * n_ya
    kl = nx // n_ya
    jl = ny // n_zb
    nz = zl * n_zb
    kc = kl // chunks

    loads = [
        pltpu.make_async_copy(a, b, load_sem.at[i])
        for i, (a, b) in enumerate(
            [(source, src), (table_x, tx), (table_y, ty), (high_z, hz), (low_z, lz)]
        )
    ]
    for load in loads:
        load.start()

    barrier = pltpu.get_barrier_semaphore()

    def greet_a(step, _):
        pl.semaphore_signal(
            barrier, inc=1, device_id={"ya": partner(ya, step, n_ya)}, device_id_type=MESH
        )
        return 0

    def greet_b(step, _):
        pl.semaphore_signal(
            barrier, inc=1, device_id={"zb": partner(zb, step, n_zb)}, device_id_type=MESH
        )
        return 0

    lax.fori_loop(1, n_ya, greet_a, 0)
    lax.fori_loop(1, n_zb, greet_b, 0)

    loads[0].wait()
    loads[1].wait()

    flat_src = src.reshape(nx * yl, zl)
    flat_first = first.reshape(nx * yl, zl)

    def x_step(pair, _):
        values = jnp.concatenate(
            [flat_src[pl.ds(2 * pair + t, nx, stride=yl), :] for t in range(2)], axis=1
        )
        modes = left_product(tx[...], values)
        for t in range(2):
            flat_first[pl.ds(2 * pair + t, nx, stride=yl), :] = modes[:, t * zl:(t + 1) * zl]
        return 0

    lax.fori_loop(0, yl // 2, x_step, 0)

    pl.semaphore_wait(barrier, n_ya + n_zb - 2)

    def copy_a(chunk, step):
        peer = partner(ya, step, n_ya)
        return pltpu.make_async_remote_copy(
            src_ref=first.at[pl.ds(peer * kl + chunk * kc, kc)],
            dst_ref=second.at[pl.ds(chunk * kc, kc), pl.ds(pl.multiple_of(ya * yl, yl), yl)],
            send_sem=send_a.at[chunk, step],
            recv_sem=recv_a.at[chunk, step],
            device_id={"ya": peer},
            device_id_type=MESH,
        )

    def arrive_a(chunk, step):
        peer = back(ya, step, n_ya)
        there = second.at[pl.ds(chunk * kc, kc), pl.ds(pl.multiple_of(peer * yl, yl), yl)]
        return pltpu.make_async_copy(there, there, recv_a.at[chunk, step])

    def copy_b(chunk, step):
        peer = partner(zb, step, n_zb)
        return pltpu.make_async_remote_copy(
            src_ref=third.at[pl.ds(chunk * kc, kc), pl.ds(pl.multiple_of(peer * jl, jl), jl)],
            dst_ref=lines.at[zb, pl.ds(chunk * kc, kc)],
            send_sem=send_b.at[chunk, step],
            recv_sem=recv_b.at[chunk, step],
            device_id={"zb": peer},
            device_id_type=MESH,
        )

    def arrive_b(chunk, step):
        there = lines.at[back(zb, step, n_zb), pl.ds(chunk * kc, kc)]
        return pltpu.make_async_copy(there, there, recv_b.at[chunk, step])

    def each_a(todo):
        lax.fori_loop(1, n_ya, lambda i, _: (todo(n_ya - i), 0)[1], 0)

    def each_b(todo):
        lax.fori_loop(1, n_zb, lambda i, _: (todo(n_zb - i), 0)[1], 0)

    def send_chunk(chunk, _):
        each_a(lambda step: copy_a(chunk, step).start())
        return 0

    lax.fori_loop(0, chunks, send_chunk, 0)

    second[:, pl.ds(pl.multiple_of(ya * yl, yl), yl), :] = first[pl.ds(ya * kl, kl)]

    loads[2].wait()
    loads[3].wait()
    loads[4].wait()

    def y_stage(chunk):
        each_a(lambda step: arrive_a(chunk, step).wait())
        width = 2 if kc % 2 == 0 else 1
        for k in range(0, kc, width):
            values = jnp.concatenate(
                [second[chunk * kc + k + t] for t in range(width)], axis=1
            )
            modes = left_product(ty[...], values)
            for t in range(width):
                third[chunk * kc + k + t] = modes[:, t * zl:(t + 1) * zl]
        each_b(lambda step: copy_b(chunk, step).start())
        lines[zb, pl.ds(chunk * kc, kc)] = third[
            pl.ds(chunk * kc, kc), pl.ds(pl.multiple_of(zb * jl, jl), jl), :
        ]

    def z_stage(chunk):
        each_b(lambda step: arrive_b(chunk, step).wait())
        values = jnp.concatenate(
            [lines[b, pl.ds(chunk * kc, kc)].reshape(kc * jl, zl) for b in range(n_zb)], axis=1
        )
        high, low = halves(values)
        dot = functools.partial(jnp.dot, preferred_element_type=jnp.float32)
        modes = dot(high, hz[...]) + dot(low, hz[...]) + dot(high, lz[...])
        out[pl.ds(chunk * kc, kc)] = modes.reshape(kc, jl, nz)

    def both(chunk, _):
        y_stage(chunk)
        z_stage(chunk - 1)
        return 0

    y_stage(0)
    lax.fori_loop(1, chunks, both, 0)
    z_stage(chunks - 1)

    def drain(chunk, _):
        each_a(lambda step: copy_a(chunk, step).wait_send())
        each_b(lambda step: copy_b(chunk, step).wait_send())
        return 0

    lax.fori_loop(0, chunks, drain, 0)


def body(n_ya, n_zb, source, symbol_x, symbol_y, symbol_z):
    nx, yl, zl = source.shape
    ny, nz = yl * n_ya, zl * n_zb
    kl, jl = nx // n_ya, ny // n_zb
    chunks = min(CHUNKS, kl)
    tables = []
    for count in (nx, ny):
        high, low = transform_table(count)
        tables.append(np.concatenate([high, high, low], axis=1))
    tables += list(transform_table(nz))
    dma = pltpu.SemaphoreType.DMA
    vmem = pltpu.VMEM
    modes = pl.pallas_call(
        functools.partial(kernel, n_ya, n_zb, chunks),
        out_shape=jax.ShapeDtypeStruct((kl, jl, nz), jnp.float32),
        in_specs=[pl.BlockSpec(memory_space=pltpu.HBM)] * 5,
        out_specs=pl.BlockSpec(memory_space=pltpu.VMEM),
        scratch_shapes=[
            vmem((nx, yl, zl), jnp.float32),
            vmem((nx, 3 * nx), jnp.bfloat16),
            vmem((ny, 3 * ny), jnp.bfloat16),
            vmem((nz, nz), jnp.bfloat16),
            vmem((nz, nz), jnp.bfloat16),
            vmem((nx, yl, zl), jnp.float32),
            vmem((kl, ny, zl), jnp.float32),
            vmem((kl, ny, zl), jnp.float32),
            vmem((n_zb, kl, jl, zl), jnp.float32),
            dma((5,)),
            dma((chunks, n_ya)),
            dma((chunks, n_ya)),
            dma((chunks, n_zb)),
            dma((chunks, n_zb)),
        ],
        compiler_params=pltpu.CompilerParams(
            collective_id=0, has_side_effects=True, vmem_limit_bytes=60 * 2**20
        ),
    )(source, *[jnp.asarray(t) for t in tables])
    part_x = lax.dynamic_slice_in_dim(symbol_x, lax.axis_index("ya") * kl, kl)
    part_y = lax.dynamic_slice_in_dim(symbol_y, lax.axis_index("zb") * jl, jl)
    symbol = part_x[:, None, None] + part_y[None, :, None] + symbol_z[None, None, :]
    return modes * lax.rsqrt(symbol)


def solution(mesh):
    placed = (P(None, "ya", "zb"), P(), P(), P())
    return jax.shard_map(
        functools.partial(body, mesh.shape["ya"], mesh.shape["zb"]),
        mesh=mesh, in_specs=placed, out_specs=P("ya", "zb", None), check_vma=False,
    )
```

time: 66.3 us -> 42.8 us (0.65)
  Pallas kernels: 0 us -> 38.8 us
  blocking collectives: 32.9 us -> 0 us
  waiting for transfers between devices: 12.7 us -> 0 us
  matrix products: 10.5 us -> 0 us
  local copies, waits for them, and re-layouts: 6.11 us -> 1.39 us
  starting transfers between devices: 3.7 us -> 0 us
  other arithmetic: 0.08 us -> 2.48 us
    pallas_call x0 -> x1, Pallas kernels: none -> 38.8 us  [body(): pl.pallas_call(functools.partial(kernel, n_ya, n_zb, chunks), out_shape=j...]
    all_to_all x1 -> x0, blocking collectives: 32.9 us -> none  [body(): lax.all_to_all(part_values, 'ya', split_axis=0, concat_axis=1, tiled=True)]
    all_to_all x1 -> x0, waiting for transfers between devices: 12.7 us -> none  [body(): lax.all_to_all(pencil_values, 'zb', split_axis=1, concat_axis=2, tiled=True)]
    dot_general x3 -> x0, matrix products: 10.5 us -> none  [transform_dim(): jnp.tensordot(values, transform_table(values.shape[dim]), axes=([dim], [0...]
    all_to_all x1 -> x0, starting transfers between devices: 3.7 us -> none  [body(): lax.all_to_all(pencil_values, 'zb', split_axis=1, concat_axis=2, tiled=True)]
    mul x0 -> x1, other arithmetic: none -> 2.41 us  [body(): return modes * lax.rsqrt(symbol)]
    unnamed x8 -> x6, local copies, waits for them, and re-layouts: 2.77 us -> 1.24 us
    transpose x1 -> x0, local copies, waits for them, and re-layouts: 1.38 us -> none  [transform_dim(): return jnp.moveaxis(moved, -1, dim)]
  transfers between devices with their start and end apart: 1 -> 0, of which waited for: 1 -> 0; matrix products, arithmetic and copies ran while one was open for 0% -> 0% of each run, Pallas kernels for 0% -> 0%
where the time goes in v1:
time: 42.8 us; the launch traced here: 42.6 us
  Pallas kernels  38.8 us (91%)
  other arithmetic  2.48 us (6%)
  local copies, waits for them, and re-layouts  1.39 us (3%)
    pallas_call x1, Pallas kernels, body(): pl.pallas_call(functools.partial(kernel, n_ya, n_zb, chunks), out_shape=j...  38.8 us
    mul x1, other arithmetic, body(): return modes * lax.rsqrt(symbol)  2.41 us
    unnamed x6, local copies, waits for them, and re-layouts  1.24 us

profile of v1, /device:TPU:0, one launch (start us, length us, event | category | flops | bytes accessed | tf_op | source)
XLA Modules:
  0.0 42.6 jit_solution(7324631967014430915)
XLA Ops:
  0.0 0.0 copy-start.1
  0.0 0.7 %copy-done.1 = f32[128]{0:T(128)S(1)} copy-done((f32[128]{0:T(128)S(1)}, f32[128]{0:T(128)}, u32[]{:S(2)}) %copy-start.1) | copy-done | bytes 536
  0.7 0.0 copy-start.2
  0.7 0.1 dynamic_slice.7
  0.7 0.6 %copy-done.2 = f32[128]{0:T(128)S(1)} copy-done((f32[128]{0:T(128)S(1)}, f32[128]{0:T(128)}, u32[]{:S(2)}) %copy-start.2) | copy-done | bytes 536
  1.3 0.1 dynamic_slice.6
  1.4 0.1 broadcast_add_fusion
  1.5 0.0 copy-start
  1.5 38.8 %shard_map.82 = f32[16,32,512]{2,1,0:T(8,128)} custom-call(f32[128,16,128]{2,1,0:T(8,128)} %source.1, bf16[128,384]{1,0:T(8,128)(2,1)} %constant.23.clone.table_x.table_y, bf16[128,384]{1,0:T(8,128)(2,1)} %constant.23.clone.table_x.table_y, bf16[512,512]{1,0:T(8,128)(2,1)} %constant.24.clone.high_z, bf16[512,512]{1,0:T(8,128)(2,1)} %constant.25.clone.low_z), custom_call_target="tpu_custom_call" | custom-call | tf_op jit(solution)/shard_map/pallas_call | solution.py:214
  40.2 0.0 copy-done
  40.2 2.4 %rsqrt_multiply_fusion = f32[16,32,512]{2,1,0:T(8,128)} fusion(f32[16,32,512]{2,1,0:T(8,128)} %shard_map.82, f32[512]{0:T(512)S(1)} %copy-done, f32[16,32]{1,0:T(8,128)S(1)} %broadcast_add_fusion), kind=kLoop, calls=%fused_computation | loop fusion | flops 524288 | bytes 2101248 | tf_op jit(solution)/shard_map/mul | solution.py:242
Async XLA Ops:
  0.0 0.7 %copy-start.1 = (f32[128]{0:T(128)S(1)}, f32[128]{0:T(128)}, u32[]{:S(2)}) copy-start(f32[128]{0:T(128)} %param.10) | copy-start | bytes 1540
  0.7 0.7 %copy-start.2 = (f32[128]{0:T(128)S(1)}, f32[128]{0:T(128)}, u32[]{:S(2)}) copy-start(f32[128]{0:T(128)} %param.9) | copy-start | bytes 1540
  1.5 38.8 %copy-start = (f32[512]{0:T(512)S(1)}, f32[512]{0:T(512)}, u32[]{:S(2)}) copy-start(f32[512]{0:T(512)} %param.11) | copy-start | bytes 6148

commit v2 on v1

v2 whole, which is shorter than its diff:
```python
import functools

import jax
import jax.numpy as jnp
import numpy as np
from jax import lax
from jax.experimental import pallas as pl
from jax.experimental.pallas import tpu as pltpu
from jax.sharding import PartitionSpec as P

MESH = pl.DeviceIdType.MESH
AHEAD = 2
SHARES = (4,4,4,2,2)


def transform_table(count):
    rank = np.arange(1, count + 1)
    angle = np.pi / (count + 1) * (rank[:, None] * rank[None, :] % (2 * count + 2))
    table = np.sqrt(2.0 / (count + 1)) * np.sin(angle)
    high = table.astype(jnp.bfloat16)
    low = (table - high.astype(np.float64)).astype(jnp.bfloat16)
    return high, low


def halves(values):
    high = values.astype(jnp.bfloat16)
    return high, (values - high.astype(jnp.float32)).astype(jnp.bfloat16)


def left_product(table3, values):
    high, low = halves(values)
    stacked = jnp.concatenate([high, low, high], axis=0)
    return jnp.dot(table3, stacked, preferred_element_type=jnp.float32)


def partners(me, count):
    if count & (count - 1):
        return (
            [lax.rem(me + step, count) for step in range(count)],
            [lax.rem(me + count - step, count) for step in range(count)],
        )
    peers, bit = [me], 1
    while bit < count:
        turn = bit * (1 - 2 * lax.rem(lax.div(me, bit), 2))
        peers += [peer + turn for peer in peers]
        bit *= 2
    return peers, peers


def kernel(
    n_ya, n_zb, bounds,
    source, table_x, table_y, high_z, low_z, symbol_x, symbol_y, symbol_z,
    out,
    src, tx, ty, hz, lz, sx, sy, sz, first, second, third, lines, column_x, base,
    load_sem, send_a, recv_a, send_b, recv_b,
):
    ya, zb = lax.axis_index("ya"), lax.axis_index("zb")
    nx, yl, zl = source.shape
    ny = yl * n_ya
    kl = nx // n_ya
    jl = ny // n_zb
    nz = zl * n_zb
    chunks = len(bounds) - 1

    barrier = pltpu.get_barrier_semaphore()

    to_a, from_a = partners(ya, n_ya)
    to_b, from_b = partners(zb, n_zb)
    for axis, peers in (("ya", to_a), ("zb", to_b)):
        for peer in reversed(peers[1:]):
            pl.semaphore_signal(barrier, inc=1, device_id={axis: peer}, device_id_type=MESH)

    loads = [
        pltpu.make_async_copy(a, b, load_sem.at[i])
        for i, (a, b) in enumerate(
            [
                (source, src), (table_x, tx), (table_y, ty), (high_z, hz), (low_z, lz),
                (symbol_x, sx), (symbol_y, sy), (symbol_z, sz),
            ]
        )
    ]
    for load in loads:
        load.start()

    loads[0].wait()
    loads[1].wait()

    flat_src = src.reshape(nx * yl, zl)
    flat_first = first.reshape(nx * yl, zl)

    def x_step(pair, _):
        values = jnp.concatenate(
            [flat_src[pl.ds(2 * pair + t, nx, stride=yl), :] for t in range(2)], axis=1
        )
        modes = left_product(tx[...], values)
        for t in range(2):
            flat_first[pl.ds(2 * pair + t, nx, stride=yl), :] = modes[:, t * zl:(t + 1) * zl]
        return 0

    lax.fori_loop(0, yl // 2, x_step, 0)

    pl.semaphore_wait(barrier, n_ya + n_zb - 2)

    def size(chunk):
        return bounds[chunk + 1] - bounds[chunk]

    def span(chunk):
        return pl.ds(bounds[chunk], size(chunk))

    def copy_a(chunk, step):
        peer = to_a[step]
        return pltpu.make_async_remote_copy(
            src_ref=first.at[pl.ds(peer * kl + bounds[chunk], size(chunk))],
            dst_ref=second.at[span(chunk), pl.ds(pl.multiple_of(ya * yl, yl), yl)],
            send_sem=send_a.at[chunk, step],
            recv_sem=recv_a.at[chunk, step],
            device_id={"ya": peer},
            device_id_type=MESH,
        )

    def arrive_a(chunk, step):
        peer = from_a[step]
        there = second.at[span(chunk), pl.ds(pl.multiple_of(peer * yl, yl), yl)]
        return pltpu.make_async_copy(there, there, recv_a.at[chunk, step])

    def copy_b(chunk, step):
        peer = to_b[step]
        return pltpu.make_async_remote_copy(
            src_ref=third.at[span(chunk), pl.ds(pl.multiple_of(peer * jl, jl), jl)],
            dst_ref=lines.at[zb, span(chunk)],
            send_sem=send_b.at[chunk, step],
            recv_sem=recv_b.at[chunk, step],
            device_id={"zb": peer},
            device_id_type=MESH,
        )

    def arrive_b(chunk, step):
        there = lines.at[from_b[step], span(chunk)]
        return pltpu.make_async_copy(there, there, recv_b.at[chunk, step])

    def each_a(todo):
        for step in range(n_ya - 1, 0, -1):
            todo(step)

    def each_b(todo):
        for step in range(n_zb - 1, 0, -1):
            todo(step)

    for chunk in range(min(AHEAD, chunks)):
        each_a(lambda step: copy_a(chunk, step).start())

    second[:, pl.ds(pl.multiple_of(ya * yl, yl), yl), :] = first[pl.ds(ya * kl, kl)]

    for load in loads[2:]:
        load.wait()

    def column(row):
        return jnp.broadcast_to(row, (zl, row.shape[1])).T

    column_x[...] = column(sx[...])
    third[0] = column(sy[...])
    own_y = third[0, pl.ds(pl.multiple_of(zb * jl, jl), jl), :]
    base[...] = jnp.concatenate([own_y] * n_zb, axis=1) + sz[...]

    def y_stage(chunk):
        each_a(lambda step: arrive_a(chunk, step).wait())
        if chunk + AHEAD < chunks:
            each_a(lambda step: copy_a(chunk + AHEAD, step).start())
        for low in range(bounds[chunk], bounds[chunk + 1], 2):
            planes = range(low, min(low + 2, bounds[chunk + 1]))
            values = jnp.concatenate([second[k] for k in planes], axis=1)
            modes = left_product(ty[...], values)
            for t, k in enumerate(planes):
                third[k] = modes[:, t * zl:(t + 1) * zl]
        each_b(lambda step: copy_b(chunk, step).start())
        lines[zb, span(chunk)] = third[
            span(chunk), pl.ds(pl.multiple_of(zb * jl, jl), jl), :
        ]

    def z_stage(chunk):
        each_b(lambda step: arrive_b(chunk, step).wait())
        values = jnp.concatenate(
            [lines[b, span(chunk)].reshape(size(chunk) * jl, zl) for b in range(n_zb)], axis=1
        )
        high, low = halves(values)
        dot = functools.partial(jnp.dot, preferred_element_type=jnp.float32)
        modes = dot(high, hz[...]) + dot(low, hz[...]) + dot(high, lz[...])
        for t in range(size(chunk)):
            k = bounds[chunk] + t
            own_x = jnp.concatenate([column_x[pl.ds(ya * kl + k, 1), :]] * n_zb, axis=1)
            out[k] = modes[t * jl:(t + 1) * jl] * lax.rsqrt(base[...] + own_x)

    for chunk in range(chunks):
        y_stage(chunk)
        if chunk:
            z_stage(chunk - 1)
    z_stage(chunks - 1)

    for chunk in range(chunks):
        each_a(lambda step: copy_a(chunk, step).wait_send())
        each_b(lambda step: copy_b(chunk, step).wait_send())


def body(n_ya, n_zb, source, symbol_x, symbol_y, symbol_z):
    nx, yl, zl = source.shape
    ny, nz = yl * n_ya, zl * n_zb
    kl, jl = nx // n_ya, ny // n_zb
    ends = np.cumsum(SHARES) * kl // sum(SHARES)
    bounds = tuple(sorted({0, *ends.tolist()}))
    chunks = len(bounds) - 1
    tables = []
    for count in (nx, ny):
        high, low = transform_table(count)
        tables.append(np.concatenate([high, high, low], axis=1))
    tables += list(transform_table(nz))
    room = 67_043_328 - 4 * kl * jl * nz - 2**18
    dma = pltpu.SemaphoreType.DMA
    vmem = pltpu.VMEM
    return pl.pallas_call(
        functools.partial(kernel, n_ya, n_zb, bounds),
        out_shape=pltpu.VMEM((kl, jl, nz), jnp.float32),
        in_specs=[pl.BlockSpec(memory_space=pltpu.HBM)] * 8,
        out_specs=pl.BlockSpec(memory_space=pltpu.VMEM),
        scratch_shapes=[
            vmem((nx, yl, zl), jnp.float32),
            vmem((nx, 3 * nx), jnp.bfloat16),
            vmem((ny, 3 * ny), jnp.bfloat16),
            vmem((nz, nz), jnp.bfloat16),
            vmem((nz, nz), jnp.bfloat16),
            vmem((1, nx), jnp.float32),
            vmem((1, ny), jnp.float32),
            vmem((1, nz), jnp.float32),
            vmem((nx, yl, zl), jnp.float32),
            vmem((kl, ny, zl), jnp.float32),
            vmem((kl, ny, zl), jnp.float32),
            vmem((n_zb, kl, jl, zl), jnp.float32),
            vmem((nx, zl), jnp.float32),
            vmem((jl, nz), jnp.float32),
            dma((8,)),
            dma((chunks, n_ya)),
            dma((chunks, n_ya)),
            dma((chunks, n_zb)),
            dma((chunks, n_zb)),
        ],
        compiler_params=pltpu.CompilerParams(
            collective_id=0, has_side_effects=True, vmem_limit_bytes=room
        ),
    )(
        source, *[jnp.asarray(t) for t in tables],
        symbol_x[None], symbol_y[None], symbol_z[None],
    )


def solution(mesh):
    placed = (P(None, "ya", "zb"), P(), P(), P())
    return jax.shard_map(
        functools.partial(body, mesh.shape["ya"], mesh.shape["zb"]),
        mesh=mesh, in_specs=placed, out_specs=P("ya", "zb", None), check_vma=False,
    )
```

time: 42.8 us -> 38.2 us (0.89)
  other arithmetic: 2.48 us -> 0 us
  Pallas kernels: 38.8 us -> 37.1 us
    mul x1 -> x0, other arithmetic: 2.41 us -> none  [body(): return modes * lax.rsqrt(symbol)]
    pallas_call x1, Pallas kernels: 38.8 us -> 37.1 us  [body(): pl.pallas_call(functools.partial(kernel, n_ya, n_zb, bounds), out_shape=p...]
    unnamed x6 -> x1, local copies, waits for them, and re-layouts: 1.24 us -> 0.97 us
where the time goes in v2:
time: 38.2 us; the launch traced here: 38 us
  Pallas kernels  37.1 us (97%)
  local copies, waits for them, and re-layouts  0.97 us (3%)
    pallas_call x1, Pallas kernels, body(): pl.pallas_call(functools.partial(kernel, n_ya, n_zb, bounds), out_shape=p...  37.1 us
    unnamed x1, local copies, waits for them, and re-layouts  0.97 us

profile of v2, /device:TPU:0, one launch (start us, length us, event | category | flops | bytes accessed | tf_op | source)
XLA Modules:
  0.0 38.0 jit_solution(15018612558918835237)
XLA Ops:
  0.0 37.1 %shard_map.82 = f32[16,32,512]{2,1,0:T(8,128)S(1)} custom-call(f32[128,16,128]{2,1,0:T(8,128)} %source.1, bf16[128,384]{1,0:T(8,128)(2,1)} %constant.6.clone.table_x.table_y, bf16[128,384]{1,0:T(8,128)(2,1)} %constant.6.clone.table_x.table_y, bf16[512,512]{1,0:T(8,128)(2,1)} %constant.7.clone.high_z, bf16[512,512]{1,0:T(8,128)(2,1)} %constant.8.clone.low_z, ...), custom_call_target="tpu_custom_call" | custom-call | tf_op jit(solution)/shard_map/pallas_call | solution.py:219
  37.1 1.0 %copy.10 = f32[16,32,512]{2,1,0:T(8,128)} copy(f32[16,32,512]{2,1,0:T(8,128)S(1)} %shard_map.82) | data formatting | bytes 2097152

commit v3 on v2

--- a/solution.py
+++ b/solution.py
@@ -10,7 +10,7 @@
 
 MESH = pl.DeviceIdType.MESH
 AHEAD = 2
-SHARES = (4,4,4,2,2)
+SHARES = (5,5,4,2)
 
 
 def transform_table(count):
@@ -52,7 +52,7 @@
     source, table_x, table_y, high_z, low_z, symbol_x, symbol_y, symbol_z,
     out,
     src, tx, ty, hz, lz, sx, sy, sz, first, second, third, lines, column_x, base,
-    load_sem, send_a, recv_a, send_b, recv_b,
+    load_sem, met, send_a, recv_a, send_b, recv_b,
 ):
     ya, zb = lax.axis_index("ya"), lax.axis_index("zb")
     nx, yl, zl = source.shape
@@ -66,9 +66,12 @@
 
     to_a, from_a = partners(ya, n_ya)
     to_b, from_b = partners(zb, n_zb)
-    for axis, peers in (("ya", to_a), ("zb", to_b)):
-        for peer in reversed(peers[1:]):
-            pl.semaphore_signal(barrier, inc=1, device_id={axis: peer}, device_id_type=MESH)
+    paired = n_ya & (n_ya - 1) == 0
+    direct = [step for step in range(1, n_ya) if not paired or step & (step - 1) == 0]
+    rounds = len(direct) - 1 if paired else 0
+    greeted = [("ya", to_a[step]) for step in reversed(direct)] + [("zb", peer) for peer in to_b[1:]]
+    for axis, peer in greeted:
+        pl.semaphore_signal(barrier, inc=1, device_id={axis: peer}, device_id_type=MESH)
 
     loads = [
         pltpu.make_async_copy(a, b, load_sem.at[i])
@@ -85,6 +88,12 @@
     loads[0].wait()
     loads[1].wait()
 
+    def tell(turn):
+        if turn < rounds:
+            pl.semaphore_signal(
+                met.at[turn], inc=1, device_id={"ya": to_a[2**turn]}, device_id_type=MESH
+            )
+
     flat_src = src.reshape(nx * yl, zl)
     flat_first = first.reshape(nx * yl, zl)
 
@@ -97,9 +106,10 @@
             flat_first[pl.ds(2 * pair + t, nx, stride=yl), :] = modes[:, t * zl:(t + 1) * zl]
         return 0
 
-    lax.fori_loop(0, yl // 2, x_step, 0)
-
-    pl.semaphore_wait(barrier, n_ya + n_zb - 2)
+    lax.fori_loop(0, yl // 2, x_step, 0, unroll=8)
+
+    pl.semaphore_wait(barrier, len(greeted))
+    tell(0)
 
     def size(chunk):
         return bounds[chunk + 1] - bounds[chunk]
@@ -138,15 +148,29 @@
         there = lines.at[from_b[step], span(chunk)]
         return pltpu.make_async_copy(there, there, recv_b.at[chunk, step])
 
+    order = [*range(n_ya // 2, n_ya), *range(n_ya // 2 - 1, 0, -1)]
+
     def each_a(todo):
-        for step in range(n_ya - 1, 0, -1):
+        for step in order:
             todo(step)
 
     def each_b(todo):
         for step in range(n_zb - 1, 0, -1):
             todo(step)
 
-    for chunk in range(min(AHEAD, chunks)):
+    heard = 0
+    for step in order:
+        need = (step - 2 ** (step.bit_length() - 1)).bit_length() if paired else 0
+        while heard < need:
+            pl.semaphore_wait(met.at[heard], 1)
+            heard += 1
+            tell(heard)
+        copy_a(0, step).start()
+    while heard < rounds:
+        pl.semaphore_wait(met.at[heard], 1)
+        heard += 1
+        tell(heard)
+    for chunk in range(1, min(AHEAD, chunks)):
         each_a(lambda step: copy_a(chunk, step).start())
 
     second[:, pl.ds(pl.multiple_of(ya * yl, yl), yl), :] = first[pl.ds(ya * kl, kl)]
@@ -237,6 +261,7 @@
             vmem((nx, zl), jnp.float32),
             vmem((jl, nz), jnp.float32),
             dma((8,)),
+            pltpu.SemaphoreType.REGULAR((max(1, n_ya.bit_length() - 2),)),
             dma((chunks, n_ya)),
             dma((chunks, n_ya)),
             dma((chunks, n_zb)),

time: 38.2 us -> 36.6 us (0.958)
  Pallas kernels: 37.1 us -> 35.5 us
    pallas_call x1, Pallas kernels: 37.1 us -> 35.5 us  [body(): pl.pallas_call(functools.partial(kernel, n_ya, n_zb, bounds), out_shape=p...]
where the time goes in v3:
time: 36.6 us; the launch traced here: 36.5 us
  Pallas kernels  35.5 us (97%)
  local copies, waits for them, and re-layouts  0.97 us (3%)
    pallas_call x1, Pallas kernels, body(): pl.pallas_call(functools.partial(kernel, n_ya, n_zb, bounds), out_shape=p...  35.5 us
    unnamed x1, local copies, waits for them, and re-layouts  0.97 us

profile of v3, /device:TPU:0, one launch (start us, length us, event | category | flops | bytes accessed | tf_op | source)
XLA Modules:
  0.0 36.5 jit_solution(13356501361493618492)
XLA Ops:
  0.0 35.5 %shard_map.82 = f32[16,32,512]{2,1,0:T(8,128)S(1)} custom-call(f32[128,16,128]{2,1,0:T(8,128)} %source.1, bf16[128,384]{1,0:T(8,128)(2,1)} %constant.6.clone.table_x.table_y, bf16[128,384]{1,0:T(8,128)(2,1)} %constant.6.clone.table_x.table_y, bf16[512,512]{1,0:T(8,128)(2,1)} %constant.7.clone.high_z, bf16[512,512]{1,0:T(8,128)(2,1)} %constant.8.clone.low_z, ...), custom_call_target="tpu_custom_call" | custom-call | tf_op jit(solution)/shard_map/pallas_call | solution.py:243
  35.5 1.0 %copy.10 = f32[16,32,512]{2,1,0:T(8,128)} copy(f32[16,32,512]{2,1,0:T(8,128)S(1)} %shard_map.82) | data formatting | bytes 2097152

commit v4 on v3

--- a/solution.py
+++ b/solution.py
@@ -73,11 +73,15 @@
     for axis, peer in greeted:
         pl.semaphore_signal(barrier, inc=1, device_id={axis: peer}, device_id_type=MESH)
 
+    rows = 8 if yl % 8 == 0 else yl
+    parts = [pl.ds(row, rows) for row in range(0, yl, rows)]
     loads = [
         pltpu.make_async_copy(a, b, load_sem.at[i])
         for i, (a, b) in enumerate(
             [
-                (source, src), (table_x, tx), (table_y, ty), (high_z, hz), (low_z, lz),
+                (table_x, tx),
+                *[(source.at[:, part], src.at[:, part]) for part in parts],
+                (table_y, ty), (high_z, hz), (low_z, lz),
                 (symbol_x, sx), (symbol_y, sy), (symbol_z, sz),
             ]
         )
@@ -86,7 +90,6 @@
         load.start()
 
     loads[0].wait()
-    loads[1].wait()
 
     def tell(turn):
         if turn < rounds:
@@ -106,7 +109,9 @@
             flat_first[pl.ds(2 * pair + t, nx, stride=yl), :] = modes[:, t * zl:(t + 1) * zl]
         return 0
 
-    lax.fori_loop(0, yl // 2, x_step, 0, unroll=8)
+    for i in range(len(parts)):
+        loads[1 + i].wait()
+        lax.fori_loop(i * rows // 2, (i + 1) * rows // 2, x_step, 0, unroll=rows // 2)
 
     pl.semaphore_wait(barrier, len(greeted))
     tell(0)
@@ -150,8 +155,10 @@
 
     order = [*range(n_ya // 2, n_ya), *range(n_ya // 2 - 1, 0, -1)]
 
-    def each_a(todo):
-        for step in order:
+    later = [*range(n_ya // 2 - 1, 0, -1), *range(n_ya // 2, n_ya)]
+
+    def each_a(todo, steps=None):
+        for step in steps or order:
             todo(step)
 
     def each_b(todo):
@@ -171,11 +178,11 @@
         heard += 1
         tell(heard)
     for chunk in range(1, min(AHEAD, chunks)):
-        each_a(lambda step: copy_a(chunk, step).start())
+        each_a(lambda step: copy_a(chunk, step).start(), later)
 
     second[:, pl.ds(pl.multiple_of(ya * yl, yl), yl), :] = first[pl.ds(ya * kl, kl)]
 
-    for load in loads[2:]:
+    for load in loads[1 + len(parts):]:
         load.wait()
 
     def column(row):
@@ -188,8 +195,6 @@
 
     def y_stage(chunk):
         each_a(lambda step: arrive_a(chunk, step).wait())
-        if chunk + AHEAD < chunks:
-            each_a(lambda step: copy_a(chunk + AHEAD, step).start())
         for low in range(bounds[chunk], bounds[chunk + 1], 2):
             planes = range(low, min(low + 2, bounds[chunk + 1]))
             values = jnp.concatenate([second[k] for k in planes], axis=1)
@@ -197,6 +202,8 @@
             for t, k in enumerate(planes):
                 third[k] = modes[:, t * zl:(t + 1) * zl]
         each_b(lambda step: copy_b(chunk, step).start())
+        if chunk + AHEAD < chunks:
+            each_a(lambda step: copy_a(chunk + AHEAD, step).start(), later)
         lines[zb, span(chunk)] = third[
             span(chunk), pl.ds(pl.multiple_of(zb * jl, jl), jl), :
         ]
@@ -260,7 +267,7 @@
             vmem((n_zb, kl, jl, zl), jnp.float32),
             vmem((nx, zl), jnp.float32),
             vmem((jl, nz), jnp.float32),
-            dma((8,)),
+            dma((7 + max(1, yl // 8),)),
             pltpu.SemaphoreType.REGULAR((max(1, n_ya.bit_length() - 2),)),
             dma((chunks, n_ya)),
             dma((chunks, n_ya)),

time: 36.6 us -> 36.5 us (level)
  no operation moved by 1% of the time
where the time goes in v4:
time: 36.5 us; the launch traced here: 36.4 us
  Pallas kernels  35.4 us (97%)
  local copies, waits for them, and re-layouts  0.97 us (3%)
    pallas_call x1, Pallas kernels, body(): pl.pallas_call(functools.partial(kernel, n_ya, n_zb, bounds), out_shape=p...  35.4 us
    unnamed x1, local copies, waits for them, and re-layouts  0.97 us

profile of v4, /device:TPU:0, one launch (start us, length us, event | category | flops | bytes accessed | tf_op | source)
XLA Modules:
  0.0 36.4 jit_solution(2447455813637656746)
XLA Ops:
  0.0 35.4 %shard_map.82 = f32[16,32,512]{2,1,0:T(8,128)S(1)} custom-call(f32[128,16,128]{2,1,0:T(8,128)} %source.1, bf16[128,384]{1,0:T(8,128)(2,1)} %constant.6.clone.table_x.table_y, bf16[128,384]{1,0:T(8,128)(2,1)} %constant.6.clone.table_x.table_y, bf16[512,512]{1,0:T(8,128)(2,1)} %constant.7.clone.high_z, bf16[512,512]{1,0:T(8,128)(2,1)} %constant.8.clone.low_z, ...), custom_call_target="tpu_custom_call" | custom-call | tf_op jit(solution)/shard_map/pallas_call | solution.py:250
  35.4 1.0 %copy.10 = f32[16,32,512]{2,1,0:T(8,128)} copy(f32[16,32,512]{2,1,0:T(8,128)S(1)} %shard_map.82) | data formatting | bytes 2097152

commit v5 on v3

--- a/solution.py
+++ b/solution.py
@@ -208,7 +208,9 @@
         )
         high, low = halves(values)
         dot = functools.partial(jnp.dot, preferred_element_type=jnp.float32)
-        modes = dot(high, hz[...]) + dot(low, hz[...]) + dot(high, lz[...])
+        both = dot(jnp.concatenate([high, low], axis=0), hz[...])
+        rows = high.shape[0]
+        modes = both[:rows] + both[rows:] + dot(high, lz[...])
         for t in range(size(chunk)):
             k = bounds[chunk] + t
             own_x = jnp.concatenate([column_x[pl.ds(ya * kl + k, 1), :]] * n_zb, axis=1)

time: 36.6 us -> 36.5 us (level)
  no operation moved by 1% of the time
where the time goes in v5:
time: 36.5 us; the launch traced here: 36.4 us
  Pallas kernels  35.4 us (97%)
  local copies, waits for them, and re-layouts  0.97 us (3%)
    pallas_call x1, Pallas kernels, body(): pl.pallas_call(functools.partial(kernel, n_ya, n_zb, bounds), out_shape=p...  35.4 us
    unnamed x1, local copies, waits for them, and re-layouts  0.97 us

profile of v5, /device:TPU:0, one launch (start us, length us, event | category | flops | bytes accessed | tf_op | source)
XLA Modules:
  0.0 36.4 jit_solution(13159165996548093813)
XLA Ops:
  0.0 35.4 %shard_map.82 = f32[16,32,512]{2,1,0:T(8,128)S(1)} custom-call(f32[128,16,128]{2,1,0:T(8,128)} %source.1, bf16[128,384]{1,0:T(8,128)(2,1)} %constant.6.clone.table_x.table_y, bf16[128,384]{1,0:T(8,128)(2,1)} %constant.6.clone.table_x.table_y, bf16[512,512]{1,0:T(8,128)(2,1)} %constant.7.clone.high_z, bf16[512,512]{1,0:T(8,128)(2,1)} %constant.8.clone.low_z, ...), custom_call_target="tpu_custom_call" | custom-call | tf_op jit(solution)/shard_map/pallas_call | solution.py:245
  35.4 1.0 %copy.10 = f32[16,32,512]{2,1,0:T(8,128)} copy(f32[16,32,512]{2,1,0:T(8,128)S(1)} %shard_map.82) | data formatting | bytes 2097152
